TPU v7x, 128 devices: a whole 4x4x4 slice. The times are simulated.
128 devices in a mesh: tiles: 32 (over x, y, core), reps: 4 (over z).
Axes of the slice: x: 4, y: 4, z: 4, core: 2. Of those that a mesh axis runs over, the one named last changes fastest.
Arguments:
- tiles_w: bfloat16 [4096, 128, 128], P('tiles'), may hold values from 0.0001 to 4
- tile_worker: int32 [4096], P('tiles'), may hold values from 0 to 15
- tile_owner: int32 [4096], P('tiles'), may hold values from 0 to 31
- owner_block: int32 [32, 32], P('tiles'), may hold values from 0 to 1
- worker_base: float32 [65536], P('tiles'), may hold values from -6 to 6
- worker_noise: float32 [65536], P('tiles'), may hold values from 0.2 to 1.5
- worker_cluster: int32 [65536], P('tiles'), may hold values from 0 to 255
- firm_base: float32 [8192], P('tiles'), may hold values from -6 to 6
- firm_noise: float32 [8192], P('tiles'), may hold values from 0.2 to 1.5
- firm_cluster: int32 [8192], P('tiles'), may hold values from 0 to 255
- signs: int32 [256, 256], P('reps'), may hold values from 0 to 1
- covariates: float32 [8192, 512], P('tiles'), may hold values from -0.0625 to 0.0625
- whitening: float32 [512, 512], replicated, may hold values from -0.25 to 0.25
Outputs:
- worker_effect: float32 [256, 65536], P('reps', 'tiles')
- firm_effect: float32 [256, 8192], P('reps', 'tiles')
- coefficients: float32 [256, 512], P('reps')
- covariance: float32 [512, 512], P('tiles')
Inputs may be any that keep to these rules, and one draw needn't show every extreme that they name: `tile_worker`: local worker block of each tile. `tile_owner`: owner of each tile's firm block. `owner_block`: firm block among the owner's 2 blocks. `signs`: a bit that gives the sign 2 b - 1.
All inputs are finite; a program needn't handle non-finite values.
Results may differ from a plain program's by a relative error of at most 0.0023.
Values may be sent and summed in bfloat16 or wider, within the bound.
No kernel may reach another device: no remote copies, remote signals or barrier semaphores. Data moves between devices by JAX's collectives and lax.ppermute only.
A program may use at most 64 MiB of HBM per device.

v0:
```python
import jax
import jax.numpy as jnp
from jax import lax
from jax.sharding import PartitionSpec as P

WORK_BLOCKS = 16
FIRM_BLOCKS = 2
SWEEPS = 6
spectral_bound = 0.8


def chebyshev_weights(sweep_count):
    weights = [1.0]
    weights.append(1.0 / (1.0 - 0.5 * spectral_bound * spectral_bound))
    while len(weights) < sweep_count:
        weights.append(1.0 / (1.0 - 0.25 * spectral_bound * spectral_bound * weights[-1]))
    return weights


def one_hot_rows(indices, row_count):
    return (indices[None, :] == jnp.arange(row_count, dtype=jnp.int32)[:, None]).astype(jnp.float32)


def wild_outcome(base_value, noise_scale, cluster, flip_table):
    clusters_hot = (
        cluster[None, :] == jnp.arange(flip_table.shape[1], dtype=jnp.int32)[:, None]
    ).astype(jnp.bfloat16)
    flip_values = jnp.dot(flip_table, clusters_hot, preferred_element_type=jnp.float32)
    return base_value[None, :] + noise_scale[None, :] * flip_values


def body(
    tiles_w,
    tile_worker,
    tile_owner,
    owner_block,
    worker_base,
    worker_noise,
    worker_cluster,
    firm_base,
    firm_noise,
    firm_cluster,
    signs,
    covariates,
    whitening,
):
    highest = lax.Precision.HIGHEST
    owners_count = lax.axis_size("tiles")
    tile_cells = tiles_w.shape[1]
    replicas_here = signs.shape[0]
    flip_table = (2 * signs - 1).astype(jnp.bfloat16)
    worker_outcome = wild_outcome(worker_base, worker_noise, worker_cluster, flip_table).reshape(
        replicas_here, WORK_BLOCKS, tile_cells
    )
    firm_outcome = wild_outcome(firm_base, firm_noise, firm_cluster, flip_table).reshape(
        replicas_here, FIRM_BLOCKS, tile_cells
    )
    row_mass = jnp.sum(tiles_w, axis=2, dtype=jnp.float32)
    col_mass = jnp.sum(tiles_w, axis=1, dtype=jnp.float32)
    worker_hot = one_hot_rows(tile_worker, WORK_BLOCKS)
    worker_scale = 1.0 + jnp.einsum("bt,tw->bw", worker_hot, row_mass, precision=highest)
    owner_hot = one_hot_rows(tile_owner, owners_count)
    my_blocks = owner_block[0]
    tile_block = tile_owner * FIRM_BLOCKS + jnp.sum(
        jnp.where(owner_hot > 0, my_blocks[:, None], 0), axis=0
    )
    dense_hot = one_hot_rows(tile_block, owners_count * FIRM_BLOCKS)
    firm_mass = lax.psum_scatter(
        jnp.einsum("nt,tf->nf", dense_hot, col_mass, precision=highest),
        "tiles",
        scatter_dimension=0,
        tiled=True,
    )
    firm_scale = 1.0 + firm_mass
    omegas = chebyshev_weights(SWEEPS)
    firm_older = jnp.zeros((replicas_here, FIRM_BLOCKS, tile_cells), jnp.float32)
    firm_newer = firm_older
    firm_now = firm_older
    worker_now = worker_outcome
    tile_firm = None
    for sweep_index in range(SWEEPS):
        if sweep_index == 0:
            worker_now = worker_outcome
        else:
            pulled = jnp.einsum(
                "twf,rtf->rtw", tiles_w, tile_firm, preferred_element_type=jnp.float32
            )
            worker_sum = jnp.einsum("bt,rtw->rbw", worker_hot, pulled, precision=highest)
            worker_now = worker_outcome - worker_sum / worker_scale[None]
        worker_round = worker_now.astype(jnp.bfloat16)
        tile_values = jnp.take(worker_round, tile_worker, axis=1)
        pushed = jnp.einsum(
            "twf,rtw->rtf", tiles_w, tile_values, preferred_element_type=jnp.float32
        )
        firm_sum = lax.psum_scatter(
            jnp.einsum("nt,rtf->rnf", dense_hot, pushed, precision=highest),
            "tiles",
            scatter_dimension=1,
            tiled=True,
        )
        firm_target = firm_outcome - firm_sum / firm_scale[None]
        firm_now = firm_older + omegas[sweep_index] * (firm_target - firm_older)
        firm_older, firm_newer = (firm_newer, firm_now)
        if sweep_index + 1 < SWEEPS:
            firm_round = firm_now.astype(jnp.bfloat16)
            every_firm = lax.all_gather(firm_round, "tiles", axis=1, tiled=True)
            tile_firm = jnp.take(every_firm, tile_block, axis=1)
    worker_effect = worker_now.reshape(replicas_here, WORK_BLOCKS * tile_cells)
    firm_flat = firm_now.reshape(replicas_here, FIRM_BLOCKS * tile_cells)
    mixing = jnp.dot(covariates, whitening.T, precision=highest)
    local_term = jnp.dot(firm_flat, mixing, precision=highest)
    summed = lax.psum(local_term, "tiles")
    share_rows = summed.shape[1] // owners_count
    own_columns = lax.dynamic_slice_in_dim(
        summed, lax.axis_index("tiles") * share_rows, share_rows, 1
    )
    moment = jnp.dot(own_columns.T, summed, precision=highest)
    covariance = lax.psum(moment, "reps") / (replicas_here * lax.axis_size("reps"))
    return (worker_effect, firm_flat, summed, covariance)


def solution(mesh):
    placed = (
        P("tiles", None, None),
        P("tiles"),
        P("tiles"),
        P("tiles", None),
        P("tiles"),
        P("tiles"),
        P("tiles"),
        P("tiles"),
        P("tiles"),
        P("tiles"),
        P("reps", None),
        P("tiles", None),
        P(),
    )
    return jax.shard_map(
        body,
        mesh=mesh,
        in_specs=placed,
        out_specs=(P("reps", "tiles"), P("reps", "tiles"), P("reps", None), P("tiles", None)),
        check_vma=False,
    )
```

profile of v0, /device:TPU:6, one launch (start us, length us, event | category | flops | bytes accessed | tf_op | source)
XLA Modules:
  0.0 1033.3 jit_solution(7390925900868006559)
XLA Ops:
  12.5 4.1 convolution_bitcast_fusion.10
  16.6 4.2 fusion.56
  20.8 2.6 copy.89
  25.3 3.5 convert_reduce_fusion
  28.9 109.8 %all-reduce = f32[64,128]{1,0:T(8,128)S(1)} all-reduce(f32[64,128]{1,0:T(8,128)S(1)} %fusion.164), channel_id=3, replica_groups=mesh['tiles'=32,'reps'=4] {'tiles'}, use_global_device_ids=true, to_apply=%region_3.0.clone | all-reduce | flops 8192 | bytes 65536
  140.8 57.8 %all-gather.6.cloned.1.call-done = bf16[64,64,128]{2,0,1:T(8,128)(2,1)} async-done(((bf16[64,2,128]{2,0,1:T(8,128)(2,1)}), bf16[64,64,128]{2,0,1:T(8,128)(2,1)}) %all-gather.6.cloned.1.call-update) | async-done | bytes 1048592 | tf_op jit(solution)/shard_map/all_gather | solution.py:106
  198.6 3.4 gather_fusion.1
  202.0 5.8 convolution_bitcast_fusion.9
  207.7 3.8 fusion.129
  213.8 4.1 convolution_bitcast_fusion.8
  217.9 4.2 fusion.59
  222.1 3.0 copy.94
  225.1 78.4 %reduce-scatter.9.cloned.1.call-done = f32[64,2,128]{2,0,1:T(8,128)} async-done(((f32[64,64,128]{2,0,1:T(8,128)}), f32[64,2,128]{2,0,1:T(8,128)}) %reduce-scatter.9.cloned.1.call-update) | async-done | bytes 65552 | tf_op jit(solution)/shard_map/reduce_scatter | solution.py:95
  305.0 43.0 %all-gather.8.cloned.1.call-done = bf16[64,64,128]{2,0,1:T(8,128)(2,1)} async-done(((bf16[64,2,128]{2,0,1:T(8,128)(2,1)}), bf16[64,64,128]{2,0,1:T(8,128)(2,1)}) %all-gather.8.cloned.1.call-update) | async-done | bytes 1048592 | tf_op jit(solution)/shard_map/all_gather | solution.py:106
  348.0 3.4 gather_fusion.3
  351.3 5.8 convolution_bitcast_fusion.7
  357.1 3.8 fusion.126
  361.0 2.2 gather_fusion.4
  363.2 4.1 convolution_bitcast_fusion.6
  367.3 4.2 fusion.62
  371.4 2.7 copy.99
  374.2 78.4 %reduce-scatter.11.cloned.1.call-done = f32[64,2,128]{2,0,1:T(8,128)} async-done(((f32[64,64,128]{2,0,1:T(8,128)}), f32[64,2,128]{2,0,1:T(8,128)}) %reduce-scatter.11.cloned.1.call-update) | async-done | bytes 65552 | tf_op jit(solution)/shard_map/reduce_scatter | solution.py:95
  454.2 43.0 %all-gather.10.cloned.1.call-done = bf16[64,64,128]{2,0,1:T(8,128)(2,1)} async-done(((bf16[64,2,128]{2,0,1:T(8,128)(2,1)}), bf16[64,64,128]{2,0,1:T(8,128)(2,1)}) %all-gather.10.cloned.1.call-update) | async-done | bytes 1048592 | tf_op jit(solution)/shard_map/all_gather | solution.py:106
  497.1 3.4 gather_fusion.5
  500.5 5.7 convolution_bitcast_fusion.5
  506.2 3.8 fusion.123
  512.3 4.1 convolution_bitcast_fusion.4
  516.4 4.2 fusion.65
  520.6 3.0 copy.104
  523.6 78.4 %reduce-scatter.13.cloned.1.call-done = f32[64,2,128]{2,0,1:T(8,128)} async-done(((f32[64,64,128]{2,0,1:T(8,128)}), f32[64,2,128]{2,0,1:T(8,128)}) %reduce-scatter.13.cloned.1.call-update) | async-done | bytes 65552 | tf_op jit(solution)/shard_map/reduce_scatter | solution.py:95
  603.5 43.1 %all-gather.12.cloned.1.call-done = bf16[64,64,128]{2,0,1:T(8,128)(2,1)} async-done(((bf16[64,2,128]{2,0,1:T(8,128)(2,1)}), bf16[64,64,128]{2,0,1:T(8,128)(2,1)}) %all-gather.12.cloned.1.call-update) | async-done | bytes 1048592 | tf_op jit(solution)/shard_map/all_gather | solution.py:106
  646.6 3.4 gather_fusion.7
  650.0 5.8 convolution_bitcast_fusion.3
  655.8 3.8 fusion.120
  661.8 4.1 convolution_bitcast_fusion.2
  665.9 4.2 fusion.68
  670.1 2.7 copy.109
  672.9 78.4 %reduce-scatter.15.cloned.1.call-done = f32[64,2,128]{2,0,1:T(8,128)} async-done(((f32[64,64,128]{2,0,1:T(8,128)}), f32[64,2,128]{2,0,1:T(8,128)}) %reduce-scatter.15.cloned.1.call-update) | async-done | bytes 65552 | tf_op jit(solution)/shard_map/reduce_scatter | solution.py:95
  752.8 43.0 %all-gather.14.cloned.1.call-done = bf16[64,64,128]{2,0,1:T(8,128)(2,1)} async-done(((bf16[64,2,128]{2,0,1:T(8,128)(2,1)}), bf16[64,64,128]{2,0,1:T(8,128)(2,1)}) %all-gather.14.cloned.1.call-update) | async-done | bytes 1048592 | tf_op jit(solution)/shard_map/all_gather | solution.py:106
  795.8 3.4 gather_fusion.9
  799.1 5.8 convolution_bitcast_fusion.1
  804.9 3.8 fusion.213
  811.0 4.1 convolution_bitcast_fusion
  815.1 4.2 fusion.71
  819.2 2.8 copy.114
  824.1 76.3 %reduce-scatter.17.cloned.1.call-done = f32[64,2,128]{2,0,1:T(8,128)} async-done(((f32[64,64,128]{2,0,1:T(8,128)}), f32[64,2,128]{2,0,1:T(8,128)}) %reduce-scatter.17.cloned.1.call-update) | async-done | bytes 65552 | tf_op jit(solution)/shard_map/reduce_scatter | solution.py:95
  903.4 102.1 %all-reduce.3.cloned.1.call-done = f32[64,512]{1,0:T(8,128)} async-done(((f32[64,512]{1,0:T(8,128)}), f32[64,512]{1,0:T(8,128)}) %all-reduce.3.cloned.1.call-update) | async-done | bytes 131088 | tf_op jit(solution)/shard_map/psum | solution.py:112
  1006.8 17.3 %psum.15 = f32[16,512]{1,0:T(8,128)S(1)} all-reduce(f32[16,512]{1,0:T(8,128)S(1)} %fusion.162), channel_id=1, replica_groups=mesh['tiles'=32,'reps'=4] {'reps'}, use_global_device_ids=true, to_apply=%region_11.14 | all-reduce | flops 8192 | bytes 65536 | tf_op jit(solution)/shard_map/psum | solution.py:118
  (89 shorter events, 32.5 us)
Async XLA Ops:
  7.2 814.9 %copy-start = (f32[512,512]{1,0:T(8,128)S(1)}, f32[512,512]{1,0:T(8,128)}, u32[]{:S(2)}) copy-start(f32[512,512]{1,0:T(8,128)} %param.29) | copy-start | bytes 3145732
  7.2 3.1 copy-start.11
  7.2 3.1 copy-start.6
  7.2 131.7 %reduce-scatter.7.cloned.1.call-start = ((), (), s32[]{:S(2)}) async-start(), calls=%async_computation.6 | async-start | bytes 2162688 | tf_op jit(solution)/shard_map/reduce_scatter | solution.py:95
  23.3 0.7 copy-start.12
  23.4 175.2 %all-gather.6.cloned.1.call-start = ((), (), s32[]{:S(2)}) async-start(), calls=%async_computation.7 | async-start | bytes 1081344 | tf_op jit(solution)/shard_map/all_gather | solution.py:106
  25.2 113.4 %copy-start.7 = (s32[64,256]{1,0:T(8,128)S(1)}, s32[64,256]{1,0:T(8,128)}, u32[]{:S(2)}) copy-start(s32[64,256]{1,0:T(8,128)} %param.27) | copy-start | bytes 196612
  25.2 113.4 %copy-start.8 = (s32[256]{0:T(256)S(1)}, s32[256]{0:T(256)}, u32[]{:S(2)}) copy-start(s32[256]{0:T(256)} %param.26) | copy-start | bytes 3076
  25.2 113.4 %copy-start.9 = (f32[256]{0:T(256)S(1)}, f32[256]{0:T(256)}, u32[]{:S(2)}) copy-start(f32[256]{0:T(256)} %param.25) | copy-start | bytes 3076
  25.3 113.4 %copy-start.10 = (f32[256]{0:T(256)S(1)}, f32[256]{0:T(256)}, u32[]{:S(2)}) copy-start(f32[256]{0:T(256)} %param.24) | copy-start | bytes 3076
  25.3 115.4 %copy-start.5 = (s32[128]{0:T(128)S(1)}, s32[128]{0:T(128)}, u32[]{:S(2)}) copy-start(s32[128]{0:T(128)} %param.18) | copy-start | bytes 1540
  140.4 163.1 %reduce-scatter.9.cloned.1.call-start = ((), (), s32[]{:S(2)}) async-start(), calls=%async_computation.8 | async-start | bytes 2162688 | tf_op jit(solution)/shard_map/reduce_scatter | solution.py:95
  225.0 122.9 %all-gather.8.cloned.1.call-start = ((), (), s32[]{:S(2)}) async-start(), calls=%async_computation.9 | async-start | bytes 1081344 | tf_op jit(solution)/shard_map/all_gather | solution.py:106
  305.0 147.6 %reduce-scatter.11.cloned.1.call-start = ((), (), s32[]{:S(2)}) async-start(), calls=%async_computation.10 | async-start | bytes 2162688 | tf_op jit(solution)/shard_map/reduce_scatter | solution.py:95
  374.2 78.4 %copy-start.2 = (f32[64,2,128]{2,0,1:T(8,128)S(1)}, f32[64,2,128]{2,0,1:T(8,128)}, u32[]{:S(2)}) copy-start(f32[64,2,128]{2,0,1:T(8,128)} %reduce-scatter.7.cloned.1.call-done) | copy-start | bytes 196612
  374.2 122.9 %all-gather.10.cloned.1.call-start = ((), (), s32[]{:S(2)}) async-start(), calls=%async_computation.11 | async-start | bytes 1081344 | tf_op jit(solution)/shard_map/all_gather | solution.py:106
  454.1 147.9 %reduce-scatter.13.cloned.1.call-start = ((), (), s32[]{:S(2)}) async-start(), calls=%async_computation.12 | async-start | bytes 2162688 | tf_op jit(solution)/shard_map/reduce_scatter | solution.py:95
  523.5 78.4 %copy-start.3 = (f32[64,2,128]{2,0,1:T(8,128)S(1)}, f32[64,2,128]{2,0,1:T(8,128)}, u32[]{:S(2)}) copy-start(f32[64,2,128]{2,0,1:T(8,128)} %reduce-scatter.9.cloned.1.call-done) | copy-start | bytes 196612
  523.6 123.1 %all-gather.12.cloned.1.call-start = ((), (), s32[]{:S(2)}) async-start(), calls=%async_computation.13 | async-start | bytes 1081344 | tf_op jit(solution)/shard_map/all_gather | solution.py:106
  603.5 147.8 %reduce-scatter.15.cloned.1.call-start = ((), (), s32[]{:S(2)}) async-start(), calls=%async_computation.14 | async-start | bytes 2162688 | tf_op jit(solution)/shard_map/reduce_scatter | solution.py:95
  672.9 122.9 %all-gather.14.cloned.1.call-start = ((), (), s32[]{:S(2)}) async-start(), calls=%async_computation.15 | async-start | bytes 1081344 | tf_op jit(solution)/shard_map/all_gather | solution.py:106
  752.8 147.7 %reduce-scatter.17.cloned.1.call-start = ((), (), s32[]{:S(2)}) async-start(), calls=%async_computation.16 | async-start | bytes 2162688 | tf_op jit(solution)/shard_map/reduce_scatter | solution.py:95
  822.0 1.0 copy-start.1
  822.0 183.5 %all-reduce.3.cloned.1.call-start = ((), (), s32[]{:S(2)}) async-start(), calls=%async_computation.17 | async-start | bytes 262144 | tf_op jit(solution)/shard_map/psum | solution.py:112
  901.3 124.9 %copy-start.4 = (f32[64,256]{1,0:T(8,128)}, f32[64,256]{1,0:T(8,128)S(1)}, u32[]{:S(2)}) copy-start(f32[64,256]{1,0:T(8,128)S(1)} %copy_bitcast_fusion.1) | copy-start | bytes 196612
Sparse Core Ops, SparseCore 0:
  23.5 80.7 reduce-scatter.6
  140.5 58.0 all-gather.5
  225.2 78.2 reduce-scatter.8
  306.1 41.7 all-gather.7
  374.3 78.2 reduce-scatter.10
  455.3 41.7 all-gather.9
  523.7 78.2 reduce-scatter.12
  604.8 41.7 all-gather.11
  673.0 78.2 reduce-scatter.14
  753.9 41.7 all-gather.13
  822.2 78.2 reduce-scatter.16
  904.1 101.3 all-reduce.2
where the time goes:
time: 1040 us; the launch traced here: 1030 us
  waiting for transfers between devices  722 us (69%)
  blocking collectives  127 us (12%)
  matrix products  103 us (10%)
  local copies, waits for them, and re-layouts  51.7 us (5%)
  between operations  15.5 us (1%)
  other arithmetic  13.9 us (1%)
    reduce_scatter x6, waiting for transfers between devices, body(): lax.psum_scatter(jnp.einsum('nt,rtf->rnf', dense_hot, pushed, precision=h...  390 us
    all_gather x5, waiting for transfers between devices, body(): every_firm = lax.all_gather(firm_round, 'tiles', axis=1, tiled=True)  230 us
    unnamed x1, blocking collectives  110 us
    psum x1, waiting for transfers between devices, body(): summed = lax.psum(local_term, 'tiles')  102 us
    dot_general x5, matrix products, body(): jnp.einsum('twf,rtf->rtw', tiles_w, tile_firm, preferred_element_type=jnp...  28.7 us
    dot_general x6, matrix products, body(): jnp.einsum('nt,rtf->rnf', dense_hot, pushed, precision=highest)  24.9 us
    dot_general x6, matrix products, body(): jnp.einsum('twf,rtw->rtf', tiles_w, tile_values, preferred_element_type=j...  24.6 us
  transfers between devices with their start and end apart: 12, of which 11 were waited for; matrix products, arithmetic and copies ran while one was open for 1% of the time, Pallas kernels for 0%

commit v1 on v0

--- a/solution.py
+++ b/solution.py
@@ -109,7 +109,7 @@
     firm_flat = firm_now.reshape(replicas_here, FIRM_BLOCKS * tile_cells)
     mixing = jnp.dot(covariates, whitening.T, precision=highest)
     local_term = jnp.dot(firm_flat, mixing, precision=highest)
-    summed = lax.psum(local_term, "tiles")
+    summed = jnp.sum(lax.all_gather(local_term, "tiles"), axis=0)
     share_rows = summed.shape[1] // owners_count
     own_columns = lax.dynamic_slice_in_dim(
         summed, lax.axis_index("tiles") * share_rows, share_rows, 1

time: 1040 us -> 985 us (0.947)
  waiting for transfers between devices: 722 us -> 665 us
    psum x1 -> x0, waiting for transfers between devices: 102 us -> none  [body(): summed = lax.psum(local_term, 'tiles')]
    all_gather x0 -> x1, waiting for transfers between devices: none -> 45.1 us  [body(): summed = jnp.sum(lax.all_gather(local_term, 'tiles'), axis=0)]
where the time goes in v1:
time: 985 us; the launch traced here: 976 us
  waiting for transfers between devices  665 us (68%)
  blocking collectives  127 us (13%)
  matrix products  102 us (10%)
  local copies, waits for them, and re-layouts  50.2 us (5%)
  other arithmetic  16.4 us (2%)
  between operations  15.5 us (2%)
    reduce_scatter x6, waiting for transfers between devices, body(): lax.psum_scatter(jnp.einsum('nt,rtf->rnf', dense_hot, pushed, precision=h...  390 us
    all_gather x5, waiting for transfers between devices, body(): every_firm = lax.all_gather(firm_round, 'tiles', axis=1, tiled=True)  230 us
    unnamed x1, blocking collectives  110 us
    all_gather x1, waiting for transfers between devices, body(): summed = jnp.sum(lax.all_gather(local_term, 'tiles'), axis=0)  45.1 us
    dot_general x5, matrix products, body(): jnp.einsum('twf,rtf->rtw', tiles_w, tile_firm, preferred_element_type=jnp...  28.8 us
    dot_general x6, matrix products, body(): jnp.einsum('nt,rtf->rnf', dense_hot, pushed, precision=highest)  24.9 us
    dot_general x6, matrix products, body(): jnp.einsum('twf,rtw->rtf', tiles_w, tile_values, preferred_element_type=j...  24.6 us
  transfers between devices with their start and end apart: 12, of which 11 were waited for; matrix products, arithmetic and copies ran while one was open for 1% of the time, Pallas kernels for 0%

profile of v1, /device:TPU:6, one launch (start us, length us, event | category | flops | bytes accessed | tf_op | source)
XLA Modules:
  0.0 976.3 jit_solution(13301707793977460149)
XLA Ops:
  12.5 4.1 convolution_bitcast_fusion.10
  16.6 4.2 fusion.56
  20.8 2.6 copy.89
  25.3 3.5 convert_reduce_fusion
  28.9 109.7 %all-reduce = f32[64,128]{1,0:T(8,128)S(1)} all-reduce(f32[64,128]{1,0:T(8,128)S(1)} %fusion.164), channel_id=4, replica_groups=mesh['tiles'=32,'reps'=4] {'tiles'}, use_global_device_ids=true, to_apply=%region_3.0.clone | all-reduce | flops 8192 | bytes 65536
  140.8 57.8 %all-gather.8.cloned.1.call-done = bf16[64,64,128]{2,0,1:T(8,128)(2,1)} async-done(((bf16[64,2,128]{2,0,1:T(8,128)(2,1)}), bf16[64,64,128]{2,0,1:T(8,128)(2,1)}) %all-gather.8.cloned.1.call-update) | async-done | bytes 1048592 | tf_op jit(solution)/shard_map/all_gather | solution.py:106
  198.6 3.4 gather_fusion.1
  202.0 5.8 convolution_bitcast_fusion.9
  207.8 3.8 fusion.129
  213.8 4.1 convolution_bitcast_fusion.8
  217.9 4.2 fusion.59
  222.1 3.0 copy.94
  225.1 78.4 %reduce-scatter.9.cloned.1.call-done = f32[64,2,128]{2,0,1:T(8,128)} async-done(((f32[64,64,128]{2,0,1:T(8,128)}), f32[64,2,128]{2,0,1:T(8,128)}) %reduce-scatter.9.cloned.1.call-update) | async-done | bytes 65552 | tf_op jit(solution)/shard_map/reduce_scatter | solution.py:95
  305.0 43.0 %all-gather.10.cloned.1.call-done = bf16[64,64,128]{2,0,1:T(8,128)(2,1)} async-done(((bf16[64,2,128]{2,0,1:T(8,128)(2,1)}), bf16[64,64,128]{2,0,1:T(8,128)(2,1)}) %all-gather.10.cloned.1.call-update) | async-done | bytes 1048592 | tf_op jit(solution)/shard_map/all_gather | solution.py:106
  348.0 3.4 gather_fusion.3
  351.4 5.8 convolution_bitcast_fusion.7
  357.2 3.8 fusion.126
  363.2 4.1 convolution_bitcast_fusion.6
  367.3 4.2 fusion.62
  371.5 2.7 copy.99
  374.3 78.4 %reduce-scatter.11.cloned.1.call-done = f32[64,2,128]{2,0,1:T(8,128)} async-done(((f32[64,64,128]{2,0,1:T(8,128)}), f32[64,2,128]{2,0,1:T(8,128)}) %reduce-scatter.11.cloned.1.call-update) | async-done | bytes 65552 | tf_op jit(solution)/shard_map/reduce_scatter | solution.py:95
  454.2 43.0 %all-gather.12.cloned.1.call-done = bf16[64,64,128]{2,0,1:T(8,128)(2,1)} async-done(((bf16[64,2,128]{2,0,1:T(8,128)(2,1)}), bf16[64,64,128]{2,0,1:T(8,128)(2,1)}) %all-gather.12.cloned.1.call-update) | async-done | bytes 1048592 | tf_op jit(solution)/shard_map/all_gather | solution.py:106
  497.2 3.4 gather_fusion.5
  500.6 5.8 convolution_bitcast_fusion.5
  506.3 3.8 fusion.123
  512.4 4.1 convolution_bitcast_fusion.4
  516.5 4.2 fusion.65
  520.6 3.0 copy.104
  523.7 78.4 %reduce-scatter.13.cloned.1.call-done = f32[64,2,128]{2,0,1:T(8,128)} async-done(((f32[64,64,128]{2,0,1:T(8,128)}), f32[64,2,128]{2,0,1:T(8,128)}) %reduce-scatter.13.cloned.1.call-update) | async-done | bytes 65552 | tf_op jit(solution)/shard_map/reduce_scatter | solution.py:95
  603.6 43.1 %all-gather.14.cloned.1.call-done = bf16[64,64,128]{2,0,1:T(8,128)(2,1)} async-done(((bf16[64,2,128]{2,0,1:T(8,128)(2,1)}), bf16[64,64,128]{2,0,1:T(8,128)(2,1)}) %all-gather.14.cloned.1.call-update) | async-done | bytes 1048592 | tf_op jit(solution)/shard_map/all_gather | solution.py:106
  646.7 3.4 gather_fusion.7
  650.1 5.8 convolution_bitcast_fusion.3
  655.8 3.8 fusion.120
  661.9 4.1 convolution_bitcast_fusion.2
  666.0 4.2 fusion.68
  670.2 2.7 copy.109
  673.0 78.4 %reduce-scatter.15.cloned.1.call-done = f32[64,2,128]{2,0,1:T(8,128)} async-done(((f32[64,64,128]{2,0,1:T(8,128)}), f32[64,2,128]{2,0,1:T(8,128)}) %reduce-scatter.15.cloned.1.call-update) | async-done | bytes 65552 | tf_op jit(solution)/shard_map/reduce_scatter | solution.py:95
  752.9 43.0 %all-gather.16.cloned.1.call-done = bf16[64,64,128]{2,0,1:T(8,128)(2,1)} async-done(((bf16[64,2,128]{2,0,1:T(8,128)(2,1)}), bf16[64,64,128]{2,0,1:T(8,128)(2,1)}) %all-gather.16.cloned.1.call-update) | async-done | bytes 1048592 | tf_op jit(solution)/shard_map/all_gather | solution.py:106
  795.8 3.4 gather_fusion.9
  799.2 5.8 convolution_bitcast_fusion.1
  805.0 3.8 fusion.213
  811.1 4.1 convolution_bitcast_fusion
  815.2 4.2 fusion.71
  819.3 2.8 copy.114
  824.2 76.3 %reduce-scatter.17.cloned.1.call-done = f32[64,2,128]{2,0,1:T(8,128)} async-done(((f32[64,64,128]{2,0,1:T(8,128)}), f32[64,2,128]{2,0,1:T(8,128)}) %reduce-scatter.17.cloned.1.call-update) | async-done | bytes 65552 | tf_op jit(solution)/shard_map/reduce_scatter | solution.py:95
  903.5 45.1 %all-gather.18.cloned.1.call-done = f32[2048,512]{1,0:T(8,128)} async-done(((f32[64,512]{1,0:T(8,128)}), f32[2048,512]{1,0:T(8,128)}) %all-gather.18.cloned.1.call-update) | async-done | bytes 4194320 | tf_op jit(solution)/shard_map/all_gather | solution.py:112
  948.5 2.5 reduce_sum.39
  951.4 17.3 %psum.7 = f32[16,512]{1,0:T(8,128)S(1)} all-reduce(f32[16,512]{1,0:T(8,128)S(1)} %fusion.162), channel_id=1, replica_groups=mesh['tiles'=32,'reps'=4] {'reps'}, use_global_device_ids=true, to_apply=%region_11.14 | all-reduce | flops 8192 | bytes 65536 | tf_op jit(solution)/shard_map/psum | solution.py:118
  (91 shorter events, 32.2 us)
Async XLA Ops:
  7.2 815.0 %copy-start = (f32[512,512]{1,0:T(8,128)S(1)}, f32[512,512]{1,0:T(8,128)}, u32[]{:S(2)}) copy-start(f32[512,512]{1,0:T(8,128)} %param.29) | copy-start | bytes 3145732
  7.2 3.1 copy-start.12
  7.2 3.1 copy-start.7
  7.2 131.7 %reduce-scatter.7.cloned.1.call-start = ((), (), s32[]{:S(2)}) async-start(), calls=%async_computation.6 | async-start | bytes 2162688 | tf_op jit(solution)/shard_map/reduce_scatter | solution.py:95
  23.3 0.7 copy-start.13
  23.4 175.3 %all-gather.8.cloned.1.call-start = ((), (), s32[]{:S(2)}) async-start(), calls=%async_computation.7 | async-start | bytes 1081344 | tf_op jit(solution)/shard_map/all_gather | solution.py:106
  25.2 113.4 %copy-start.8 = (s32[64,256]{1,0:T(8,128)S(1)}, s32[64,256]{1,0:T(8,128)}, u32[]{:S(2)}) copy-start(s32[64,256]{1,0:T(8,128)} %param.27) | copy-start | bytes 196612
  25.2 113.4 %copy-start.9 = (s32[256]{0:T(256)S(1)}, s32[256]{0:T(256)}, u32[]{:S(2)}) copy-start(s32[256]{0:T(256)} %param.26) | copy-start | bytes 3076
  25.3 113.4 %copy-start.10 = (f32[256]{0:T(256)S(1)}, f32[256]{0:T(256)}, u32[]{:S(2)}) copy-start(f32[256]{0:T(256)} %param.25) | copy-start | bytes 3076
  25.3 113.4 %copy-start.11 = (f32[256]{0:T(256)S(1)}, f32[256]{0:T(256)}, u32[]{:S(2)}) copy-start(f32[256]{0:T(256)} %param.24) | copy-start | bytes 3076
  25.3 115.4 %copy-start.6 = (s32[128]{0:T(128)S(1)}, s32[128]{0:T(128)}, u32[]{:S(2)}) copy-start(s32[128]{0:T(128)} %param.18) | copy-start | bytes 1540
  140.4 163.1 %reduce-scatter.9.cloned.1.call-start = ((), (), s32[]{:S(2)}) async-start(), calls=%async_computation.8 | async-start | bytes 2162688 | tf_op jit(solution)/shard_map/reduce_scatter | solution.py:95
  225.1 122.9 %all-gather.10.cloned.1.call-start = ((), (), s32[]{:S(2)}) async-start(), calls=%async_computation.9 | async-start | bytes 1081344 | tf_op jit(solution)/shard_map/all_gather | solution.py:106
  305.0 147.7 %reduce-scatter.11.cloned.1.call-start = ((), (), s32[]{:S(2)}) async-start(), calls=%async_computation.10 | async-start | bytes 2162688 | tf_op jit(solution)/shard_map/reduce_scatter | solution.py:95
  374.2 78.4 %copy-start.3 = (f32[64,2,128]{2,0,1:T(8,128)S(1)}, f32[64,2,128]{2,0,1:T(8,128)}, u32[]{:S(2)}) copy-start(f32[64,2,128]{2,0,1:T(8,128)} %reduce-scatter.7.cloned.1.call-done) | copy-start | bytes 196612
  374.3 122.9 %all-gather.12.cloned.1.call-start = ((), (), s32[]{:S(2)}) async-start(), calls=%async_computation.11 | async-start | bytes 1081344 | tf_op jit(solution)/shard_map/all_gather | solution.py:106
  454.2 147.9 %reduce-scatter.13.cloned.1.call-start = ((), (), s32[]{:S(2)}) async-start(), calls=%async_computation.12 | async-start | bytes 2162688 | tf_op jit(solution)/shard_map/reduce_scatter | solution.py:95
  523.6 78.4 %copy-start.4 = (f32[64,2,128]{2,0,1:T(8,128)S(1)}, f32[64,2,128]{2,0,1:T(8,128)}, u32[]{:S(2)}) copy-start(f32[64,2,128]{2,0,1:T(8,128)} %reduce-scatter.9.cloned.1.call-done) | copy-start | bytes 196612
  523.6 123.1 %all-gather.14.cloned.1.call-start = ((), (), s32[]{:S(2)}) async-start(), calls=%async_computation.13 | async-start | bytes 1081344 | tf_op jit(solution)/shard_map/all_gather | solution.py:106
  603.6 147.8 %reduce-scatter.15.cloned.1.call-start = ((), (), s32[]{:S(2)}) async-start(), calls=%async_computation.14 | async-start | bytes 2162688 | tf_op jit(solution)/shard_map/reduce_scatter | solution.py:95
  672.9 122.9 %all-gather.16.cloned.1.call-start = ((), (), s32[]{:S(2)}) async-start(), calls=%async_computation.15 | async-start | bytes 1081344 | tf_op jit(solution)/shard_map/all_gather | solution.py:106
  752.8 147.7 %reduce-scatter.17.cloned.1.call-start = ((), (), s32[]{:S(2)}) async-start(), calls=%async_computation.16 | async-start | bytes 2162688 | tf_op jit(solution)/shard_map/reduce_scatter | solution.py:95
  822.1 1.0 copy-start.2
  822.1 126.4 %all-gather.18.cloned.1.call-start = ((), (), s32[]{:S(2)}) async-start(), calls=%async_computation.17 | async-start | bytes 4325376 | tf_op jit(solution)/shard_map/all_gather | solution.py:112
  901.4 49.7 %copy-start.5 = (f32[64,256]{1,0:T(8,128)}, f32[64,256]{1,0:T(8,128)S(1)}, u32[]{:S(2)}) copy-start(f32[64,256]{1,0:T(8,128)S(1)} %copy_bitcast_fusion.1) | copy-start | bytes 196612
  951.1 18.2 %copy-start.1 = (f32[64,512]{1,0:T(8,128)}, f32[64,512]{1,0:T(8,128)S(1)}, u32[]{:S(2)}) copy-start(f32[64,512]{1,0:T(8,128)S(1)} %reduce_sum.39) | copy-start | bytes 393220
Sparse Core Ops, SparseCore 0:
  23.5 80.8 reduce-scatter.6
  140.5 58.0 all-gather.7
  225.2 78.2 reduce-scatter.8
  306.2 41.7 all-gather.9
  374.4 78.2 reduce-scatter.10
  455.4 41.7 all-gather.11
  523.8 78.2 reduce-scatter.12
  604.9 41.7 all-gather.13
  673.0 78.2 reduce-scatter.14
  754.0 41.7 all-gather.15
  822.2 78.2 reduce-scatter.16
  903.2 45.2 all-gather.17
